TPU v7x, 32 devices: a whole 2x2x4 slice. The times are simulated.
32 devices in a mesh: gz: 2 (over core), dp: 16 (over z, y, x).
Axes of the slice: x: 2, y: 2, z: 4, core: 2. Of those that a mesh axis runs over, the one named last changes fastest.
Arguments:
- inputs: bfloat16 [16, 32, 16, 8, 128], P('dp', None, 'gz'), may hold values from -6 to 6
- kernel_one: bfloat16 [32, 32, 3, 3, 3], replicated, may hold values from -0.21875 to 0.21875
- kernel_two: bfloat16 [32, 32, 3, 3, 3], replicated, may hold values from -0.21875 to 0.21875
- cotangent: bfloat16 [16, 32, 16, 8, 128], P('dp', None, 'gz'), may hold values from -12 to 12
Outputs:
- input_grad: bfloat16 [16, 32, 16, 8, 128], P('dp', None, 'gz')
- kernel_one_grad: float32 [32, 32, 3, 3, 3], replicated
- kernel_two_grad: float32 [32, 32, 3, 3, 3], replicated
All inputs are finite; a program needn't handle non-finite values.
Results may differ from a plain program's by a relative error of at most 0.006.
Values may be sent and summed in bfloat16 or wider, within the bound.
A program may use at most 64 MiB of HBM per device.

v0:
```python
import functools
import math

import jax
import jax.numpy as jnp
from jax import lax
from jax.experimental import pallas as pl
from jax.experimental.pallas import tpu as pltpu
from jax.sharding import PartitionSpec as P

MESH = pl.DeviceIdType.MESH
F32 = jnp.float32
BF16 = jnp.bfloat16
TAPS = [(plane, col) for plane in range(3) for col in range(3)]
NN = (((1,), (0,)), ((), ()))
NT = (((1,), (1,)), ((), ()))


def dot(a, b, dims=NN):
    return lax.dot_general(a, b, dims, preferred_element_type=F32)


def iota(shape, dim):
    return lax.broadcasted_iota(jnp.int32, shape, dim)


def one_hot(mask):
    return jnp.where(mask, 1.0, 0.0).astype(BF16)


def sigmoid(v):
    return 0.5 * jnp.tanh(0.5 * v) + 0.5


def kernel(
    sizes,
    factor,
    x_hbm,
    w1_hbm,
    w2_hbm,
    cot_hbm,
    res_ref,
    sums_ref,
    x_ref,
    w1_ref,
    w2_ref,
    cot_ref,
    s_in,
    s_hid,
    s_g2,
    s_g1,
    wcat,
    slope,
    bands,
    packed,
    arrived,
    full,
    halo_send,
    halo_recv,
    rs_send,
    rs_recv,
    ag_send,
    ag_recv,
    load_sem,
):
    gz_count, dp_count, owners = sizes
    chan, depth, height, width = x_ref.shape
    rows = chan * height
    count = gz_count * dp_count
    gz = lax.axis_index("gz")
    dp = lax.axis_index("dp")
    me = gz * dp_count + dp

    def place(dev):
        return {"gz": dev // dp_count, "dp": lax.rem(dev, dp_count)}

    loads = [
        pltpu.make_async_copy(src, dst, load_sem.at[i])
        for i, (src, dst) in enumerate(
            ((w1_hbm, w1_ref), (x_hbm, x_ref), (w2_hbm, w2_ref), (cot_hbm, cot_ref))
        )
    ]
    for copy in loads:
        copy.start()

    barrier = pltpu.get_barrier_semaphore()

    def greet(k, carry):
        dev = lax.rem(me + k, count)
        pl.semaphore_signal(barrier, inc=1, device_id=place(dev), device_id_type=MESH)
        return carry

    lax.fori_loop(1, count, greet, 0)

    r, l = iota((rows, rows), 0), iota((rows, rows), 1)
    to_rows = one_hot((r // chan == l % height) & (r % chan == l // height))

    def shifts(s, p, value):
        lane = iota(value.shape, 1)
        s[0, p] = jnp.where(lane == 0, 0.0, pltpu.roll(value, 1, 1)).astype(BF16)
        s[2, p] = jnp.where(lane == width - 1, 0.0, pltpu.roll(value, width - 1, 1)).astype(BF16)

    def put(s, p, value):
        s[1, p] = value.astype(BF16)
        shifts(s, p, value)

    def up_copy(n, s):
        return pltpu.make_async_remote_copy(
            src_ref=s.at[1, depth],
            dst_ref=s.at[1, 0],
            send_sem=halo_send.at[n, 0],
            recv_sem=halo_recv.at[n, 0],
            device_id={"gz": gz + 1, "dp": dp},
            device_id_type=MESH,
        )

    def down_copy(n, s):
        return pltpu.make_async_remote_copy(
            src_ref=s.at[1, 1],
            dst_ref=s.at[1, depth + 1],
            send_sem=halo_send.at[n, 1],
            recv_sem=halo_recv.at[n, 1],
            device_id={"gz": gz - 1, "dp": dp},
            device_id_type=MESH,
        )

    def send_halo(n, s):
        @pl.when(gz < gz_count - 1)
        def _():
            up_copy(n, s).start()

        @pl.when(gz > 0)
        def _():
            down_copy(n, s).start()

    def take_halo(n, s):
        @pl.when(gz > 0)
        def _():
            up_copy(n, s).wait_recv()

        @pl.when(gz == 0)
        def _():
            s[1, 0] = jnp.zeros((rows, width), BF16)

        @pl.when(gz < gz_count - 1)
        def _():
            down_copy(n, s).wait_recv()

        @pl.when(gz == gz_count - 1)
        def _():
            s[1, depth + 1] = jnp.zeros((rows, width), BF16)

        for p in (0, depth + 1):
            shifts(s, p, s[1, p].astype(F32))

    def raw(ref, p):
        return ref[:, p].astype(F32).reshape(rows, width).astype(BF16)

    edges = sorted({0, depth - 1})
    inner = [p for p in range(depth) if p not in edges]
    groups = [edges] + [inner[i : i + 2] for i in range(0, len(inner), 2)]

    def lanes(parts):
        return parts[0] if len(parts) == 1 else jnp.concatenate(parts, axis=1)

    def load(ref, planes):
        value = dot(to_rows, lanes([raw(ref, p) for p in planes]))
        return [value[:, i * width : (i + 1) * width] for i in range(len(planes))]

    def conv(n, s, planes):
        window = jnp.concatenate(
            [lanes([s[col, p + plane] for p in planes]) for plane, col in TAPS], axis=0
        )
        value = dot(wcat[n], window)
        return [value[:, i * width : (i + 1) * width] for i in range(len(planes))]

    pack = 4 * chan
    er, el = iota((chan, pack), 0), iota((chan, pack), 1)
    eye = one_hot(iota((chan, chan), 0) == iota((chan, chan), 1))
    blank = jnp.zeros((chan, chan), BF16)
    sr, sl = iota((pack, rows), 0), iota((pack, rows), 1)

    def forward(ref):
        base = None
        for off in range(3):
            tall = jnp.concatenate([ref[9 * a + 3 * off + b] for a, b in TAPS], axis=0)
            piece = dot(tall, one_hot(el == er + off * chan))
            base = piece if base is None else base + piece
        return [base.astype(BF16)]

    def backward(ref):
        pieces = []
        for a, b in TAPS:
            tall = jnp.concatenate(
                [ref[26 - (9 * a + 3 * off + b)] for off in range(3)] + [blank], axis=0
            )
            pieces.append(dot(eye, tall, NT).astype(BF16))
        return pieces

    def spread(first, pieces):
        base = jnp.concatenate(pieces, axis=0)
        for y in range(height):
            pick = one_hot(
                (sr % chan == sl % chan)
                & (sl // chan == y - 1 + sr // chan)
                & (sr < 3 * chan)
            )
            placed = dot(base, pick).astype(BF16)
            for at in range(base.shape[0] // chan):
                n, t = first + at // 9, at % 9
                wcat[n, y * chan : (y + 1) * chan, t * rows : (t + 1) * rows] = placed[
                    at * chan : (at + 1) * chan
                ]

    def scatter_terms(j):
        def step(k, carry):
            dev = lax.rem(me + k, count)

            @pl.when(dev < owners)
            def _():
                pltpu.make_async_remote_copy(
                    src_ref=packed.at[j, dev],
                    dst_ref=arrived.at[j, count - 1 - k],
                    send_sem=rs_send.at[j],
                    recv_sem=rs_recv.at[j],
                    device_id=place(dev),
                    device_id_type=MESH,
                ).start()

            return carry

        lax.fori_loop(1, count, step, 0)

    def wait_for(ref, sem):
        pltpu.make_async_copy(ref, ref, sem).wait()

    def gather_terms(j):
        @pl.when(me < owners)
        def _():
            wait_for(arrived.at[j], rs_recv.at[j])
            total = jnp.sum(arrived[j].astype(F32), axis=0) + packed[j, me].astype(F32)
            full[j, me] = (total * factor).astype(BF16)

            def step(k, carry):
                dev = lax.rem(me + k, count)
                pltpu.make_async_remote_copy(
                    src_ref=full.at[j, me],
                    dst_ref=full.at[j, me],
                    send_sem=ag_send.at[j],
                    recv_sem=ag_recv.at[j],
                    device_id=place(dev),
                    device_id_type=MESH,
                ).start()
                return carry

            lax.fori_loop(1, count, step, 0)

    def finish_terms(j):
        @pl.when(me < owners)
        def _():
            wait_for(full.at[j, pl.ds(0, owners - 1)], ag_recv.at[j])
            wait_for(packed.at[j, pl.ds(0, owners - 1)], rs_send.at[j])
            wait_for(arrived.at[j], ag_send.at[j])

        @pl.when(me >= owners)
        def _():
            wait_for(full.at[j, pl.ds(0, owners)], ag_recv.at[j])
            wait_for(packed.at[j, pl.ds(0, owners)], rs_send.at[j])

        sums_ref[j] = full[j].astype(F32).reshape(owners * full.shape[2], 8, 128)[:27]

    qr, ql = iota((4 * rows, 128), 0), iota((4 * rows, 128), 1)
    gather_rows = one_hot((qr // rows == ql // chan) & (qr % chan == ql % chan))

    def terms(j, s, s_grad):
        grad = lanes([s_grad[1, p + 1] for p in range(depth)])
        block = iota((chan, rows), 1) // chan
        for plane, col in TAPS:
            window = lanes([s[col, p + plane] for p in range(depth)])
            value = dot(grad, window, NT)
            for off in range(3):
                band = jnp.zeros((chan, rows), F32)
                for y in range(height):
                    if 0 <= y + off - 1 < height:
                        part = value[y * chan : (y + 1) * chan]
                        band = jnp.where(block == y + off - 1, part, band)
                t = plane * 9 + off * 3 + col
                for g in range(4):
                    bands[t * 8 : (t + 1) * 8, g * rows : (g + 1) * rows] = band[
                        g * 8 : (g + 1) * 8
                    ]
        value = bands[...]
        high = value.astype(BF16)
        low = (value - high.astype(F32)).astype(BF16)
        total = (dot(high, gather_rows) + dot(low, gather_rows)).reshape(27, 8, 128)
        tiles = packed.shape[2]
        for t in range(27):
            packed[j, t // tiles, t % tiles] = total[t].astype(BF16)

    if owners * packed.shape[2] > 27:
        packed[...] = jnp.zeros_like(packed)

    def first_layer(planes):
        for p, pre in zip(planes, conv(0, s_in, planes)):
            sig = sigmoid(pre)
            slope[p] = sig * (1.0 + pre * (1.0 - sig))
            put(s_hid, p + 1, pre * sig)

    def second_layer(planes):
        for p, pre, cot in zip(planes, conv(1, s_hid, planes), load(cot_ref, planes)):
            sig = sigmoid(pre)
            put(s_g2, p + 1, cot * (sig * (1.0 + pre * (1.0 - sig))))

    def second_back(planes):
        for p, value in zip(planes, conv(2, s_g2, planes)):
            put(s_g1, p + 1, value * slope[p])

    loads[0].wait()
    spread(0, forward(w1_ref))
    loads[1].wait()
    for planes in groups:
        for p, value in zip(planes, load(x_ref, planes)):
            put(s_in, p + 1, value)
    for planes in groups[1:]:
        first_layer(planes)
    pl.semaphore_wait(barrier, count - 1)
    send_halo(0, s_in)
    for copy in loads[2:]:
        copy.wait()
    spread(1, forward(w2_ref))
    take_halo(0, s_in)
    first_layer(groups[0])
    send_halo(1, s_hid)
    for planes in groups[1:]:
        second_layer(planes)
    spread(2, backward(w2_ref) + backward(w1_ref))
    take_halo(1, s_hid)
    second_layer(groups[0])
    send_halo(2, s_g2)
    terms(1, s_hid, s_g2)
    scatter_terms(1)
    take_halo(2, s_g2)
    for i, planes in enumerate(groups):
        second_back(planes)
        if i == 0:
            send_halo(3, s_g1)
    terms(0, s_in, s_g1)
    scatter_terms(0)
    gather_terms(1)
    take_halo(3, s_g1)
    for planes in groups:
        for p, value in zip(planes, conv(3, s_g1, planes)):
            res_ref[p] = value.astype(BF16)
    gather_terms(0)
    finish_terms(1)
    finish_terms(0)

    for n, s in enumerate((s_in, s_hid, s_g2, s_g1)):

        @pl.when(gz < gz_count - 1)
        def _():
            up_copy(n, s).wait_send()

        @pl.when(gz > 0)
        def _():
            down_copy(n, s).wait_send()


def unpack(res_ref, sums_ref, out_ref, g1_ref, g2_ref):
    chan, depth, height, width = out_ref.shape
    rows = chan * height
    for j, ref in enumerate((g1_ref, g2_ref)):
        for g in range(4):
            ref[:, g * 8 : (g + 1) * 8, :] = sums_ref[j, :, :, g * chan : (g + 1) * chan]
    r, l = iota((rows, rows), 0), iota((rows, rows), 1)
    to_chan = one_hot((r // height == l % chan) & (r % height == l // chan))
    for at in range(0, depth, 2):
        planes = range(at, min(at + 2, depth))
        value = dot(to_chan, jnp.concatenate([res_ref[p] for p in planes], axis=1))
        for i, p in enumerate(planes):
            part = value[:, i * width : (i + 1) * width]
            out_ref[:, p] = part.reshape(chan, height, width).astype(BF16)


def solution(mesh):
    gz_count, dp_count = mesh.shape["gz"], mesh.shape["dp"]
    count = gz_count * dp_count

    def local(inputs, kernel_one, kernel_two, cotangent):
        _, chan, depth, height, width = inputs.shape
        rows = chan * height
        cells = dp_count * gz_count * depth * height * width
        tiles = -(-27 // count)
        owners = -(-27 // tiles)
        taps = lambda k: k.transpose(2, 3, 4, 0, 1).reshape(27, chan, chan)
        slab = pltpu.VMEM((3, depth + 2, rows, width), BF16)
        vmem = pl.BlockSpec(memory_space=pltpu.VMEM)
        res, sums = pl.pallas_call(
            functools.partial(kernel, (gz_count, dp_count, owners), 1.0 / math.sqrt(cells)),
            out_shape=(
                jax.ShapeDtypeStruct((depth, rows, width), BF16),
                jax.ShapeDtypeStruct((2, 27, 8, 128), F32),
            ),
            in_specs=[pl.BlockSpec(memory_space=pl.ANY)] * 4,
            out_specs=(vmem, vmem),
            scratch_shapes=[
                pltpu.VMEM((chan, depth, height, width), BF16),
                pltpu.VMEM((27, chan, chan), BF16),
                pltpu.VMEM((27, chan, chan), BF16),
                pltpu.VMEM((chan, depth, height, width), BF16),
                slab,
                slab,
                slab,
                slab,
                pltpu.VMEM((4, rows, 9 * rows), BF16),
                pltpu.VMEM((depth, rows, width), F32),
                pltpu.VMEM((27 * 8, 4 * rows), F32),
                pltpu.VMEM((2, owners, tiles, 8, 128), BF16),
                pltpu.VMEM((2, count - 1, tiles, 8, 128), BF16),
                pltpu.VMEM((2, owners, tiles, 8, 128), BF16),
                pltpu.SemaphoreType.DMA((4, 2)),
                pltpu.SemaphoreType.DMA((4, 2)),
                pltpu.SemaphoreType.DMA((2,)),
                pltpu.SemaphoreType.DMA((2,)),
                pltpu.SemaphoreType.DMA((2,)),
                pltpu.SemaphoreType.DMA((2,)),
                pltpu.SemaphoreType.DMA((4,)),
            ],
            compiler_params=pltpu.CompilerParams(collective_id=0, has_side_effects=True),
        )(inputs[0], taps(kernel_one), taps(kernel_two), cotangent[0])
        out, g1, g2 = pl.pallas_call(
            unpack,
            out_shape=(
                jax.ShapeDtypeStruct((chan, depth, height, width), BF16),
                jax.ShapeDtypeStruct((27, chan, chan), F32),
                jax.ShapeDtypeStruct((27, chan, chan), F32),
            ),
            in_specs=[vmem] * 2,
            out_specs=(vmem, vmem, vmem),
        )(res, sums)
        back = lambda g: g.reshape(3, 3, 3, chan, chan).transpose(3, 4, 0, 1, 2)
        return out[None], back(g1), back(g2)

    return jax.shard_map(
        local,
        mesh=mesh,
        in_specs=(P("dp", None, "gz", None, None), P(), P(), P("dp", None, "gz", None, None)),
        out_specs=(P("dp", None, "gz", None, None), P(), P()),
        check_vma=False,
    )
```

profile of v0, /device:TPU:0, one launch (start us, length us, event | category | flops | bytes accessed | tf_op | source)
XLA Modules:
  0.0 33.2 jit_solution(441215826583323848)
XLA Ops:
  0.6 30.1 %shard_map.67 = (bf16[8,256,128]{2,1,0:T(8,128)(2,1)}, f32[2,27,8,128]{3,2,1,0:T(8,128)}) custom-call(bf16[32,8,8,128]{3,2,1,0:T(8,128)(2,1)} %bitcast.15, bf16[27,32,32]{2,1,0:T(8,128)(2,1)} %bitcast.17, bf16[27,32,32]{2,1,0:T(8,128)(2,1)} %bitcast.18, bf16[32,8,8,128]{3,2,1,0:T(8,128)(2,1)} %bitcast.16), custom_call_target="tpu_custom_call" | custom-call | tf_op jit(solution)/shard_map/pallas_call | solution.py:398
  30.8 2.4 %shard_map.68 = (bf16[32,8,8,128]{3,2,1,0:T(8,128)(2,1)}, f32[27,32,32]{2,1,0:T(8,128)}, f32[27,32,32]{2,1,0:T(8,128)}) custom-call(bf16[8,256,128]{2,1,0:T(8,128)(2,1)} %get-tuple-element.8.res_ref, f32[2,27,8,128]{3,2,1,0:T(8,128)} %get-tuple-element.9.sums_ref), custom_call_target="tpu_custom_call" | custom-call | tf_op jit(solution)/shard_map/pallas_call | solution.py:431
where the time goes:
time: 33.3 us; the launch traced here: 33.2 us
  Pallas kernels  32.6 us (98%)
  between operations  0.64 us (2%)
    pallas_call x1, Pallas kernels, local(): pl.pallas_call(functools.partial(kernel, (gz_count, dp_count, owners), 1....  30.1 us
    pallas_call x1, Pallas kernels, local(): pl.pallas_call(unpack, out_shape=(jax.ShapeDtypeStruct((chan, depth, heig...  2.43 us

commit v1 on v0

v1 whole, which is shorter than its diff:
```python
import functools
import math

import jax
import jax.numpy as jnp
from jax import lax
from jax.experimental import pallas as pl
from jax.experimental.pallas import tpu as pltpu
from jax.sharding import PartitionSpec as P

MESH = pl.DeviceIdType.MESH
F32 = jnp.float32
BF16 = jnp.bfloat16
TAPS = [(plane, col) for plane in range(3) for col in range(3)]
NN = (((1,), (0,)), ((), ()))
NT = (((1,), (1,)), ((), ()))
UNROLL_UP_TO = 64


def dot(a, b, dims=NN):
    return lax.dot_general(a, b, dims, preferred_element_type=F32)


def iota(shape, dim):
    return lax.broadcasted_iota(jnp.int32, shape, dim)


def one_hot(mask):
    return jnp.where(mask, 1.0, 0.0).astype(BF16)


def sigmoid(v):
    return 0.5 * jnp.tanh(0.5 * v) + 0.5


def kernel(
    sizes,
    factor,
    x_hbm,
    w1_hbm,
    w2_hbm,
    cot_hbm,
    out_ref,
    sums_ref,
    x_ref,
    w1_ref,
    w2_ref,
    cot_ref,
    s_in,
    s_hid,
    s_g2,
    s_g1,
    wcat,
    slope,
    perm,
    packed,
    arrived,
    full,
    halo_send,
    halo_recv,
    rs_send,
    rs_recv,
    ag_send,
    ag_recv,
    load_sem,
):
    gz_count, dp_count, owners = sizes
    chan, depth, height, width = x_ref.shape
    rows = chan * height
    half = height // 2
    part_rows = half * chan
    pack = 4 * chan
    count = gz_count * dp_count
    gz = lax.axis_index("gz")
    dp = lax.axis_index("dp")
    me = gz * dp_count + dp

    loads = [
        pltpu.make_async_copy(src, dst, load_sem.at[i])
        for i, (src, dst) in enumerate(
            ((w1_hbm, w1_ref), (x_hbm, x_ref), (w2_hbm, w2_ref), (cot_hbm, cot_ref))
        )
    ]
    for copy in loads:
        copy.start()

    barrier = pltpu.get_barrier_semaphore()
    quarter = max(dp_count // 4, 1)
    offsets = [(g, d) for g in range(gz_count) for d in range(dp_count) if g or d]
    offsets.sort(key=lambda o: (0, 2, 1, 2)[o[1] // quarter % 4] * -1)

    def each_peer(act):
        if count <= UNROLL_UP_TO:
            for slot, (g, d) in enumerate(offsets):
                act(slot, lax.rem(gz + g, gz_count), lax.rem(dp + d, dp_count))
        else:

            def step(k, carry):
                dev = lax.rem(me + k, count)
                act(k - 1, dev // dp_count, lax.rem(dev, dp_count))
                return carry

            lax.fori_loop(1, count, step, 0)

    def greet(slot, to_gz, to_dp):
        pl.semaphore_signal(
            barrier, inc=1, device_id={"gz": to_gz, "dp": to_dp}, device_id_type=MESH
        )

    each_peer(greet)

    slabs = (s_in, s_hid, s_g2, s_g1)

    @pl.when(gz == 0)
    def _():
        for s in slabs:
            s[:, 0] = jnp.zeros((3, rows, width), BF16)

    @pl.when(gz == gz_count - 1)
    def _():
        for s in slabs:
            s[:, depth + 1] = jnp.zeros((3, rows, width), BF16)

    r, l = iota((rows, rows), 0), iota((rows, rows), 1)
    perm[0] = one_hot((r // chan == l % height) & (r % chan == l // height))
    perm[1] = one_hot((r // height == l % chan) & (r % height == l // chan))

    lane_of = iota((part_rows, width), 1)
    not_first, not_last = lane_of != 0, lane_of != width - 1

    def put(s, p, h, value):
        at = pl.ds(h * part_rows, part_rows)
        s[1, p, at] = value.astype(BF16)
        s[0, p, at] = jnp.where(not_first, pltpu.roll(value, 1, 1), 0.0).astype(BF16)
        s[2, p, at] = jnp.where(not_last, pltpu.roll(value, width - 1, 1), 0.0).astype(BF16)

    def up_copy(n):
        return pltpu.make_async_remote_copy(
            src_ref=slabs[n].at[:, depth],
            dst_ref=slabs[n].at[:, 0],
            send_sem=halo_send.at[n, 0],
            recv_sem=halo_recv.at[n, 0],
            device_id={"gz": gz + 1, "dp": dp},
            device_id_type=MESH,
        )

    def down_copy(n):
        return pltpu.make_async_remote_copy(
            src_ref=slabs[n].at[:, 1],
            dst_ref=slabs[n].at[:, depth + 1],
            send_sem=halo_send.at[n, 1],
            recv_sem=halo_recv.at[n, 1],
            device_id={"gz": gz - 1, "dp": dp},
            device_id_type=MESH,
        )

    def send_halo(n):
        @pl.when(gz < gz_count - 1)
        def _():
            up_copy(n).start()

        @pl.when(gz > 0)
        def _():
            down_copy(n).start()

    def take_halo(n):
        @pl.when(gz > 0)
        def _():
            up_copy(n).wait_recv()

        @pl.when(gz < gz_count - 1)
        def _():
            down_copy(n).wait_recv()

    def raw(ref, p):
        return ref[:, p].astype(F32).reshape(rows, width).astype(BF16)

    edges = sorted({0, depth - 1})
    inner = [p for p in range(depth) if p not in edges]
    groups = [edges] + [inner[i : i + 2] for i in range(0, len(inner), 2)]

    def lanes(parts):
        return parts[0] if len(parts) == 1 else jnp.concatenate(parts, axis=1)

    def split(value, planes):
        return [value[:, i * width : (i + 1) * width] for i in range(len(planes))]

    def load(ref, planes):
        return split(dot(perm[0], lanes([raw(ref, p) for p in planes])), planes)

    def conv(n, s, planes, h):
        first = h * (half - 1) * chan
        span = lambda at, size: [
            lanes([s[col, p + plane, at : at + size] for p in planes]) for plane, col in TAPS
        ]
        window = jnp.concatenate(
            span(first, part_rows) + span(first + part_rows, chan), axis=0
        )
        return split(dot(wcat[n, h, :, : 9 * (part_rows + chan)], window), planes)

    lane32 = iota((chan, pack), 1)
    quad = lane32 // chan
    er, el = iota((chan, pack), 0), lane32
    eye = one_hot(iota((chan, chan), 0) == iota((chan, chan), 1))
    blank = jnp.zeros((chan, chan), BF16)

    def forward(ref):
        base = None
        for off in range(3):
            tall = jnp.concatenate([ref[9 * a + 3 * off + b] for a, b in TAPS], axis=0)
            piece = dot(tall, one_hot(el == er + off * chan))
            base = piece if base is None else base + piece
        return [base[t * chan : (t + 1) * chan] for t in range(9)]

    def backward(ref):
        pieces = []
        for a, b in TAPS:
            tall = jnp.concatenate(
                [ref[26 - (9 * a + 3 * off + b)] for off in range(3)] + [blank], axis=0
            )
            pieces.append(dot(eye, tall, NT))
        return pieces

    def place_weights(n, pieces):
        extra = 9 * pack
        turned = []
        for t, b0 in enumerate(pieces):
            b1, b2, b3 = (pltpu.roll(b0, i * chan, 1) for i in (1, 2, 3))
            turned.append((b0, b1, b2, b3))
            mid = jnp.where(quad >= 2, b2, 0.0).astype(BF16)
            a0, a1 = b0.astype(BF16), b1.astype(BF16)
            low = jnp.where(quad < 2, b3, 0.0).astype(BF16)
            high = jnp.where(quad == 3, b3, 0.0).astype(BF16)
            for h, blocks in enumerate(((low, a0, a1, mid), (a0, a1, mid, high))):
                for y, block in enumerate(blocks):
                    wcat[n, h, y * chan : (y + 1) * chan, t * pack : (t + 1) * pack] = block

        def gather(off, q):
            value = jnp.zeros((chan, pack), F32)
            for t in range(4 * q, min(4 * q + 4, 9)):
                value = jnp.where(quad == t % 4, turned[t][(t - off) % 4], value)
            return value.astype(BF16)

        for q in range(3):
            at = slice(extra + q * pack, extra + (q + 1) * pack)
            last = gather(2, q)
            wcat[n, 0, 3 * chan : 4 * chan, at] = last
            wcat[n, 1, 2 * chan : 3 * chan, at] = last
            wcat[n, 1, 3 * chan : 4 * chan, at] = gather(1, q)

    for n in range(4):
        at = slice(9 * pack, 12 * pack)
        wcat[n, 0, : 3 * chan, at] = jnp.zeros((3 * chan, 3 * pack), BF16)
        wcat[n, 1, : 2 * chan, at] = jnp.zeros((2 * chan, 3 * pack), BF16)

    def scatter_terms(j):
        def send(slot, to_gz, to_dp):
            dev = to_gz * dp_count + to_dp

            @pl.when(dev < owners)
            def _():
                pltpu.make_async_remote_copy(
                    src_ref=packed.at[j, dev],
                    dst_ref=arrived.at[j, slot],
                    send_sem=rs_send.at[j],
                    recv_sem=rs_recv.at[j],
                    device_id={"gz": to_gz, "dp": to_dp},
                    device_id_type=MESH,
                ).start()

        each_peer(send)

    def wait_for(ref, sem):
        pltpu.make_async_copy(ref, ref, sem).wait()

    def gather_terms(j):
        @pl.when(me < owners)
        def _():
            wait_for(arrived.at[j], rs_recv.at[j])
            total = jnp.sum(arrived[j].astype(F32), axis=0) + packed[j, me].astype(F32)
            full[j, me] = total.astype(BF16)

            def send(slot, to_gz, to_dp):
                pltpu.make_async_remote_copy(
                    src_ref=full.at[j, me],
                    dst_ref=full.at[j, me],
                    send_sem=ag_send.at[j],
                    recv_sem=ag_recv.at[j],
                    device_id={"gz": to_gz, "dp": to_dp},
                    device_id_type=MESH,
                ).start()

            each_peer(send)

    def finish_terms(j):
        @pl.when(me < owners)
        def _():
            wait_for(full.at[j, pl.ds(0, owners - 1)], ag_recv.at[j])
            wait_for(packed.at[j, pl.ds(0, owners - 1)], rs_send.at[j])
            wait_for(arrived.at[j], ag_send.at[j])

        @pl.when(me >= owners)
        def _():
            wait_for(full.at[j, pl.ds(0, owners)], ag_recv.at[j])
            wait_for(packed.at[j, pl.ds(0, owners)], rs_send.at[j])

        sums_ref[j] = full[j]

    pr, pc = iota((3 * chan, 8 * chan), 0), iota((3 * chan, 8 * chan), 1)
    choose = one_hot(pc == (2 - pr // chan) * 2 * chan + pr % chan)

    def terms(j, s, s_grad):
        def source(pairs, plane, rel):
            cells = []
            for m in pairs:
                y = 2 * m + rel
                for p in range(depth):
                    if 0 <= y < height:
                        cells.append(s[1, p + plane, y * chan : (y + 1) * chan])
                    else:
                        cells.append(jnp.zeros((chan, width), BF16))
            return lanes(cells)

        def grad(pairs, col):
            return lanes(
                [
                    s_grad[col, p + 1, 2 * m * chan : (2 * m + 2) * chan]
                    for m in pairs
                    for p in range(depth)
                ]
            )

        def product(pairs):
            streamed = [source(pairs, plane, rel) for plane in range(3) for rel in range(-1, 3)]
            held = [grad(pairs, col) for col in (0, 1, 2, 1)]
            return dot(jnp.concatenate(streamed, axis=0), jnp.concatenate(held, axis=0), NT)

        values = [product(range(height // 4)), product(range(height // 4, height // 2))]

        def block(at, i):
            cells = slice(i * pack, (i + 1) * pack)
            return values[0][at : at + chan, cells] * factor + values[1][at : at + chan, cells] * factor

        blocks = []
        for plane in range(3):
            for off in range(3):
                at = (plane * 4 + off) * chan
                blocks.append(
                    lanes(
                        [
                            block(at, i) + pltpu.roll(block(at + chan, i), 3 * chan, 1)
                            for i in range(2)
                        ]
                    ).astype(BF16)
                )
        blocks.append(jnp.zeros((3 * chan, 8 * chan), BF16))
        turned = dot(choose, jnp.concatenate(blocks, axis=0), NT)
        tail = turned[:, 2 * pack :]
        tail = (
            tail[:chan]
            + pltpu.roll(tail[chan : 2 * chan], chan, 1)
            + pltpu.roll(tail[2 * chan :], 2 * chan, 1)
        )
        tiles = packed.shape[2]
        sources = [
            turned[8 * i : 8 * i + 8, g * pack : (g + 1) * pack]
            for i in range(3 * chan // 8)
            for g in range(2)
        ] + [tail[8 * i : 8 * i + 8] for i in range(chan // 8)]
        for t, tile in enumerate(sources):
            packed[j, t // tiles, t % tiles] = tile.astype(BF16)

    if owners * packed.shape[2] > 28:
        packed[...] = jnp.zeros_like(packed)

    def first_layer(planes):
        for h in range(2):
            at = pl.ds(h * part_rows, part_rows)
            for p, pre in zip(planes, conv(0, s_in, planes, h)):
                sig = sigmoid(pre)
                slope[p, at] = sig * (1.0 + pre * (1.0 - sig))
                put(s_hid, p + 1, h, pre * sig)

    def second_layer(planes):
        cots = load(cot_ref, planes)
        for h in range(2):
            for p, pre, cot in zip(planes, conv(1, s_hid, planes, h), cots):
                sig = sigmoid(pre)
                cot = cot[h * part_rows : (h + 1) * part_rows]
                put(s_g2, p + 1, h, cot * (sig * (1.0 + pre * (1.0 - sig))))

    def second_back(planes):
        for h in range(2):
            at = pl.ds(h * part_rows, part_rows)
            for p, value in zip(planes, conv(2, s_g2, planes, h)):
                put(s_g1, p + 1, h, value * slope[p, at])

    def first_back(planes):
        value = jnp.concatenate(
            [lanes(conv(3, s_g1, planes, h)).astype(BF16) for h in range(2)], axis=0
        )
        for p, part in zip(planes, split(dot(perm[1], value), planes)):
            out_ref[:, p] = part.reshape(chan, height, width).astype(BF16)

    loads[0].wait()
    place_weights(0, forward(w1_ref))
    loads[1].wait()
    for planes in groups:
        for p, value in zip(planes, load(x_ref, planes)):
            for h in range(2):
                put(s_in, p + 1, h, value[h * part_rows : (h + 1) * part_rows])
    for planes in groups[1:]:
        first_layer(planes)
    pl.semaphore_wait(barrier, count - 1)
    send_halo(0)
    for copy in loads[2:]:
        copy.wait()
    place_weights(1, forward(w2_ref))
    place_weights(2, backward(w2_ref))
    take_halo(0)
    first_layer(groups[0])
    send_halo(1)
    for planes in groups[1:]:
        second_layer(planes)
    place_weights(3, backward(w1_ref))
    take_halo(1)
    second_layer(groups[0])
    send_halo(2)
    terms(1, s_hid, s_g2)
    scatter_terms(1)
    take_halo(2)
    for i, planes in enumerate(groups):
        second_back(planes)
        if i == 0:
            send_halo(3)
    terms(0, s_in, s_g1)
    scatter_terms(0)
    take_halo(3)
    for planes in groups:
        first_back(planes)
    gather_terms(1)
    gather_terms(0)
    finish_terms(1)
    finish_terms(0)

    for n in range(4):

        @pl.when(gz < gz_count - 1)
        def _():
            up_copy(n).wait_send()

        @pl.when(gz > 0)
        def _():
            down_copy(n).wait_send()


def unpack(out_ref, sums_ref, out_hbm, g1_hbm, g2_hbm, grads_ref, sems):
    chan = out_ref.shape[0]
    store_out = pltpu.make_async_copy(out_ref, out_hbm, sems.at[2])
    store_out.start()
    store = [
        pltpu.make_async_copy(grads_ref.at[j], g, sems.at[j]) for j, g in enumerate((g1_hbm, g2_hbm))
    ]
    groups = chan // 8
    for j in range(2):
        for kx in range(3):
            for o in range(groups):
                at = slice(8 * o, 8 * o + 8)
                for g in range(2):
                    tile = sums_ref[j, (kx * groups + o) * 2 + g].astype(F32)
                    for i in range(4):
                        t = (4 * g + i) * 3 + kx
                        grads_ref[j, t, at] = tile[:, i * chan : (i + 1) * chan]
        for o in range(groups):
            tile = sums_ref[j, 6 * groups + o].astype(F32)
            for kx in range(3):
                grads_ref[j, 24 + kx, 8 * o : 8 * o + 8] = tile[:, kx * chan : (kx + 1) * chan]
        store[j].start()
    for move in store:
        move.wait()
    store_out.wait()


def solution(mesh):
    gz_count, dp_count = mesh.shape["gz"], mesh.shape["dp"]
    count = gz_count * dp_count

    def local(inputs, kernel_one, kernel_two, cotangent):
        _, chan, depth, height, width = inputs.shape
        rows = chan * height
        cells = dp_count * gz_count * depth * height * width
        tiles = -(-28 // count)
        owners = -(-28 // tiles)
        taps = lambda k: k.transpose(2, 3, 4, 0, 1).reshape(27, chan, chan)
        slab = pltpu.VMEM((3, depth + 2, rows, width), BF16)
        vmem = pl.BlockSpec(memory_space=pltpu.VMEM)
        anywhere = pl.BlockSpec(memory_space=pl.ANY)
        out, sums = pl.pallas_call(
            functools.partial(kernel, (gz_count, dp_count, owners), 1.0 / math.sqrt(cells)),
            out_shape=(
                pltpu.VMEM((chan, depth, height, width), BF16),
                pltpu.VMEM((2, owners, tiles, 8, 128), BF16),
            ),
            in_specs=[anywhere] * 4,
            out_specs=(vmem, vmem),
            scratch_shapes=[
                pltpu.VMEM((chan, depth, height, width), BF16),
                pltpu.VMEM((27, chan, chan), BF16),
                pltpu.VMEM((27, chan, chan), BF16),
                pltpu.VMEM((chan, depth, height, width), BF16),
                slab,
                slab,
                slab,
                slab,
                pltpu.VMEM((4, 2, rows // 2, 12 * 4 * chan), BF16),
                pltpu.VMEM((depth, rows, width), F32),
                pltpu.VMEM((2, rows, rows), BF16),
                pltpu.VMEM((2, owners, tiles, 8, 128), BF16),
                pltpu.VMEM((2, count - 1, tiles, 8, 128), BF16),
                pltpu.VMEM((2, owners, tiles, 8, 128), BF16),
                pltpu.SemaphoreType.DMA((4, 2)),
                pltpu.SemaphoreType.DMA((4, 2)),
                pltpu.SemaphoreType.DMA((2,)),
                pltpu.SemaphoreType.DMA((2,)),
                pltpu.SemaphoreType.DMA((2,)),
                pltpu.SemaphoreType.DMA((2,)),
                pltpu.SemaphoreType.DMA((4,)),
            ],
            compiler_params=pltpu.CompilerParams(collective_id=0, has_side_effects=True),
        )(inputs[0], taps(kernel_one), taps(kernel_two), cotangent[0])
        sums = sums.reshape(2, owners * tiles, 8, 128)
        out, sums = (pltpu.with_memory_space_constraint(v, pltpu.VMEM) for v in (out, sums))
        out, g1, g2 = pl.pallas_call(
            unpack,
            out_shape=(
                jax.ShapeDtypeStruct((chan, depth, height, width), BF16),
                jax.ShapeDtypeStruct((27, chan, chan), F32),
                jax.ShapeDtypeStruct((27, chan, chan), F32),
            ),
            in_specs=[vmem] * 2,
            out_specs=(anywhere,) * 3,
            scratch_shapes=[
                pltpu.VMEM((2, 27, chan, chan), F32),
                pltpu.SemaphoreType.DMA((3,)),
            ],
        )(out, sums)
        back = lambda g: g.reshape(3, 3, 3, chan, chan).transpose(3, 4, 0, 1, 2)
        return out[None], back(g1), back(g2)

    return jax.shard_map(
        local,
        mesh=mesh,
        in_specs=(P("dp", None, "gz", None, None), P(), P(), P("dp", None, "gz", None, None)),
        out_specs=(P("dp", None, "gz", None, None), P(), P()),
        check_vma=False,
    )
```

time: 33.3 us -> 26.2 us (0.79)
  Pallas kernels: 32.6 us -> 25.4 us
    pallas_call x1, Pallas kernels: 30.1 us -> 24.3 us  [local(): pl.pallas_call(functools.partial(kernel, (gz_count, dp_count, owners), 1....]
    pallas_call x1, Pallas kernels: 2.43 us -> 1.11 us  [local(): pl.pallas_call(unpack, out_shape=(jax.ShapeDtypeStruct((chan, depth, heig...]
where the time goes in v1:
time: 26.2 us; the launch traced here: 26 us
  Pallas kernels  25.4 us (97%)
  between operations  0.64 us (2%)
    pallas_call x1, Pallas kernels, local(): pl.pallas_call(functools.partial(kernel, (gz_count, dp_count, owners), 1....  24.3 us
    pallas_call x1, Pallas kernels, local(): pl.pallas_call(unpack, out_shape=(jax.ShapeDtypeStruct((chan, depth, heig...  1.11 us

profile of v1, /device:TPU:0, one launch (start us, length us, event | category | flops | bytes accessed | tf_op | source)
XLA Modules:
  0.0 26.0 jit_solution(11365383732049247950)
XLA Ops:
  0.6 24.3 %shard_map.67 = (bf16[32,8,8,128]{3,2,1,0:T(8,128)(2,1)S(1)}, bf16[2,28,1,8,128]{4,3,2,1,0:T(8,128)(2,1)S(1)}) custom-call(bf16[32,8,8,128]{3,2,1,0:T(8,128)(2,1)} %bitcast.17, bf16[27,32,32]{2,1,0:T(8,128)(2,1)} %bitcast.19, bf16[27,32,32]{2,1,0:T(8,128)(2,1)} %bitcast.20, bf16[32,8,8,128]{3,2,1,0:T(8,128)(2,1)} %bitcast.18), custom_call_target="tpu_custom_call" | custom-call | tf_op jit(solution)/shard_map/pallas_call | solution.py:498
  24.9 1.1 %shard_map.68 = (bf16[32,8,8,128]{3,2,1,0:T(8,128)(2,1)}, f32[27,32,32]{2,1,0:T(8,128)}, f32[27,32,32]{2,1,0:T(8,128)}) custom-call(bf16[32,8,8,128]{3,2,1,0:T(8,128)(2,1)S(1)} %get-tuple-element.8.out_ref, bf16[2,28,8,128]{3,2,1,0:T(8,128)(2,1)S(1)} %bitcast.16), custom_call_target="tpu_custom_call" | custom-call | tf_op jit(solution)/shard_map/pallas_call | solution.py:533

commit v2 on v1

--- a/solution.py
+++ b/solution.py
@@ -53,6 +53,7 @@
     wcat,
     slope,
     perm,
+    sums_acc,
     packed,
     arrived,
     full,
@@ -64,7 +65,7 @@
     ag_recv,
     load_sem,
 ):
-    gz_count, dp_count, owners = sizes
+    gz_count, dp_count, owners, own = sizes
     chan, depth, height, width = x_ref.shape
     rows = chan * height
     half = height // 2
@@ -85,14 +86,24 @@
         copy.start()
 
     barrier = pltpu.get_barrier_semaphore()
-    quarter = max(dp_count // 4, 1)
-    offsets = [(g, d) for g in range(gz_count) for d in range(dp_count) if g or d]
-    offsets.sort(key=lambda o: (0, 2, 1, 2)[o[1] // quarter % 4] * -1)
+    outer = 4 if dp_count % 4 == 0 else 1
+    inner_count = dp_count // outer
+    dp_out, dp_in = dp // inner_count, lax.rem(dp, inner_count)
+    offsets = [
+        (g, a, b)
+        for a in sorted(range(outer), key=lambda a: -min(a, outer - a))
+        for b in reversed(range(inner_count))
+        for g in range(gz_count)
+        if g or a or b
+    ]
 
     def each_peer(act):
         if count <= UNROLL_UP_TO:
-            for slot, (g, d) in enumerate(offsets):
-                act(slot, lax.rem(gz + g, gz_count), lax.rem(dp + d, dp_count))
+            to_gz = [lax.rem(gz + g, gz_count) for g in range(gz_count)]
+            to_out = [lax.rem(dp_out + a, outer) * inner_count for a in range(outer)]
+            to_in = [lax.rem(dp_in + b, inner_count) for b in range(inner_count)]
+            for slot, (g, a, b) in enumerate(offsets):
+                act(slot, to_gz[g], to_out[a] + to_in[b])
         else:
 
             def step(k, carry):
@@ -101,6 +112,17 @@
                 return carry
 
             lax.fori_loop(1, count, step, 0)
+
+    own_gz, own_low, own_count = own
+
+    def rank_of(at_dp):
+        return at_dp - own_low
+
+    def is_owner(at_gz, at_dp):
+        inside = (at_dp >= own_low) & (at_dp < own_low + min(own_count, owners))
+        return inside & (at_gz == own_gz)
+
+    rank, owner = rank_of(dp), is_owner(gz, dp)
 
     def greet(slot, to_gz, to_dp):
         pl.semaphore_signal(
@@ -255,12 +277,10 @@
 
     def scatter_terms(j):
         def send(slot, to_gz, to_dp):
-            dev = to_gz * dp_count + to_dp
-
-            @pl.when(dev < owners)
+            @pl.when(is_owner(to_gz, to_dp))
             def _():
                 pltpu.make_async_remote_copy(
-                    src_ref=packed.at[j, dev],
+                    src_ref=packed.at[j, rank_of(to_dp)],
                     dst_ref=arrived.at[j, slot],
                     send_sem=rs_send.at[j],
                     recv_sem=rs_recv.at[j],
@@ -274,16 +294,16 @@
         pltpu.make_async_copy(ref, ref, sem).wait()
 
     def gather_terms(j):
-        @pl.when(me < owners)
+        @pl.when(owner)
         def _():
             wait_for(arrived.at[j], rs_recv.at[j])
-            total = jnp.sum(arrived[j].astype(F32), axis=0) + packed[j, me].astype(F32)
-            full[j, me] = total.astype(BF16)
+            total = jnp.sum(arrived[j].astype(F32), axis=0) + packed[j, rank].astype(F32)
+            full[j, rank] = total.astype(BF16)
 
             def send(slot, to_gz, to_dp):
                 pltpu.make_async_remote_copy(
-                    src_ref=full.at[j, me],
-                    dst_ref=full.at[j, me],
+                    src_ref=full.at[j, rank],
+                    dst_ref=full.at[j, rank],
                     send_sem=ag_send.at[j],
                     recv_sem=ag_recv.at[j],
                     device_id={"gz": to_gz, "dp": to_dp},
@@ -293,13 +313,13 @@
             each_peer(send)
 
     def finish_terms(j):
-        @pl.when(me < owners)
+        @pl.when(owner)
         def _():
             wait_for(full.at[j, pl.ds(0, owners - 1)], ag_recv.at[j])
             wait_for(packed.at[j, pl.ds(0, owners - 1)], rs_send.at[j])
             wait_for(arrived.at[j], ag_send.at[j])
 
-        @pl.when(me >= owners)
+        @pl.when(jnp.logical_not(owner))
         def _():
             wait_for(full.at[j, pl.ds(0, owners)], ag_recv.at[j])
             wait_for(packed.at[j, pl.ds(0, owners)], rs_send.at[j])
@@ -309,12 +329,14 @@
     pr, pc = iota((3 * chan, 8 * chan), 0), iota((3 * chan, 8 * chan), 1)
     choose = one_hot(pc == (2 - pr // chan) * 2 * chan + pr % chan)
 
-    def terms(j, s, s_grad):
+    halves = [range(height // 4), range(height // 4, height // 2)]
+
+    def products(s, s_grad, planes):
         def source(pairs, plane, rel):
             cells = []
             for m in pairs:
                 y = 2 * m + rel
-                for p in range(depth):
+                for p in planes:
                     if 0 <= y < height:
                         cells.append(s[1, p + plane, y * chan : (y + 1) * chan])
                     else:
@@ -326,20 +348,31 @@
                 [
                     s_grad[col, p + 1, 2 * m * chan : (2 * m + 2) * chan]
                     for m in pairs
-                    for p in range(depth)
+                    for p in planes
                 ]
             )
 
-        def product(pairs):
+        values = []
+        for pairs in halves:
             streamed = [source(pairs, plane, rel) for plane in range(3) for rel in range(-1, 3)]
             held = [grad(pairs, col) for col in (0, 1, 2, 1)]
-            return dot(jnp.concatenate(streamed, axis=0), jnp.concatenate(held, axis=0), NT)
-
-        values = [product(range(height // 4)), product(range(height // 4, height // 2))]
+            values.append(
+                dot(jnp.concatenate(streamed, axis=0), jnp.concatenate(held, axis=0), NT)
+            )
+        return values
+
+    def add_terms(j, s, s_grad, planes, first=False):
+        one, two = products(s, s_grad, planes)
+        value = one * factor + two * factor
+        sums_acc[j] = value if first else sums_acc[j] + value
+
+    def end_terms(j, s, s_grad, planes):
+        one, two = products(s, s_grad, planes)
 
         def block(at, i):
             cells = slice(i * pack, (i + 1) * pack)
-            return values[0][at : at + chan, cells] * factor + values[1][at : at + chan, cells] * factor
+            rest = one[at : at + chan, cells] * factor + two[at : at + chan, cells] * factor
+            return sums_acc[j, at : at + chan, cells] + rest
 
         blocks = []
         for plane in range(3):
@@ -402,6 +435,9 @@
         for p, part in zip(planes, split(dot(perm[1], value), planes)):
             out_ref[:, p] = part.reshape(chan, height, width).astype(BF16)
 
+    ring = lambda k: sorted({k, depth - 1 - k})
+    core = [p for p in range(2, depth - 2)]
+    core = [core[i : i + 2] for i in range(0, len(core), 2)]
     loads[0].wait()
     place_weights(0, forward(w1_ref))
     loads[1].wait()
@@ -409,35 +445,45 @@
         for p, value in zip(planes, load(x_ref, planes)):
             for h in range(2):
                 put(s_in, p + 1, h, value[h * part_rows : (h + 1) * part_rows])
-    for planes in groups[1:]:
+    for copy in loads[2:]:
+        copy.wait()
+    for i, planes in enumerate(groups[1:]):
         first_layer(planes)
+        if i == 0:
+            place_weights(1, forward(w2_ref))
     pl.semaphore_wait(barrier, count - 1)
     send_halo(0)
-    for copy in loads[2:]:
-        copy.wait()
-    place_weights(1, forward(w2_ref))
-    place_weights(2, backward(w2_ref))
+    for i, planes in enumerate(core):
+        second_layer(planes)
+        if i == 0:
+            place_weights(2, backward(w2_ref))
+    add_terms(1, s_hid, s_g2, core[0], True)
     take_halo(0)
-    first_layer(groups[0])
+    first_layer(ring(0))
     send_halo(1)
-    for planes in groups[1:]:
-        second_layer(planes)
-    place_weights(3, backward(w1_ref))
+    for planes in core[1:]:
+        add_terms(1, s_hid, s_g2, planes)
+    second_layer(ring(1))
+    for planes in core:
+        second_back(planes)
     take_halo(1)
-    second_layer(groups[0])
+    second_layer(ring(0))
     send_halo(2)
-    terms(1, s_hid, s_g2)
+    for i, planes in enumerate(core):
+        add_terms(0, s_in, s_g1, planes, i == 0)
+    second_back(ring(1))
+    end_terms(1, s_hid, s_g2, ring(0) + ring(1))
     scatter_terms(1)
     take_halo(2)
-    for i, planes in enumerate(groups):
-        second_back(planes)
-        if i == 0:
-            send_halo(3)
-    terms(0, s_in, s_g1)
+    second_back(ring(0))
+    send_halo(3)
+    end_terms(0, s_in, s_g1, ring(0) + ring(1))
     scatter_terms(0)
+    place_weights(3, backward(w1_ref))
+    for planes in groups[1:]:
+        first_back(planes)
     take_halo(3)
-    for planes in groups:
-        first_back(planes)
+    first_back(ring(0))
     gather_terms(1)
     gather_terms(0)
     finish_terms(1)
@@ -489,14 +535,16 @@
         _, chan, depth, height, width = inputs.shape
         rows = chan * height
         cells = dp_count * gz_count * depth * height * width
-        tiles = -(-28 // count)
+        own_count = dp_count // 2 if dp_count % 4 == 0 else dp_count
+        own_low = (dp_count - own_count) // 2
+        tiles = -(-28 // own_count)
         owners = -(-28 // tiles)
         taps = lambda k: k.transpose(2, 3, 4, 0, 1).reshape(27, chan, chan)
         slab = pltpu.VMEM((3, depth + 2, rows, width), BF16)
         vmem = pl.BlockSpec(memory_space=pltpu.VMEM)
         anywhere = pl.BlockSpec(memory_space=pl.ANY)
         out, sums = pl.pallas_call(
-            functools.partial(kernel, (gz_count, dp_count, owners), 1.0 / math.sqrt(cells)),
+            functools.partial(kernel, (gz_count, dp_count, owners, (gz_count - 1, own_low, own_count)), 1.0 / math.sqrt(cells)),
             out_shape=(
                 pltpu.VMEM((chan, depth, height, width), BF16),
                 pltpu.VMEM((2, owners, tiles, 8, 128), BF16),
@@ -515,6 +563,7 @@
                 pltpu.VMEM((4, 2, rows // 2, 12 * 4 * chan), BF16),
                 pltpu.VMEM((depth, rows, width), F32),
                 pltpu.VMEM((2, rows, rows), BF16),
+                pltpu.VMEM((2, 12 * chan, 8 * chan), F32),
                 pltpu.VMEM((2, owners, tiles, 8, 128), BF16),
                 pltpu.VMEM((2, count - 1, tiles, 8, 128), BF16),
                 pltpu.VMEM((2, owners, tiles, 8, 128), BF16),

time: 26.2 us -> 23.7 us (0.905)
  Pallas kernels: 25.4 us -> 22.9 us
    pallas_call x1, Pallas kernels: 24.3 us -> 21.8 us  [local(): pl.pallas_call(functools.partial(kernel, (gz_count, dp_count, owners, (gz...]
where the time goes in v2:
time: 23.7 us; the launch traced here: 23.6 us
  Pallas kernels  22.9 us (97%)
  between operations  0.64 us (3%)
    pallas_call x1, Pallas kernels, local(): pl.pallas_call(functools.partial(kernel, (gz_count, dp_count, owners, (gz...  21.8 us
    pallas_call x1, Pallas kernels, local(): pl.pallas_call(unpack, out_shape=(jax.ShapeDtypeStruct((chan, depth, heig...  1.11 us

profile of v2, /device:TPU:0, one launch (start us, length us, event | category | flops | bytes accessed | tf_op | source)
XLA Modules:
  0.0 23.6 jit_solution(5175793989368407585)
XLA Ops:
  0.6 21.8 %shard_map.67 = (bf16[32,8,8,128]{3,2,1,0:T(8,128)(2,1)S(1)}, bf16[2,7,4,8,128]{4,3,2,1,0:T(8,128)(2,1)S(1)}) custom-call(bf16[32,8,8,128]{3,2,1,0:T(8,128)(2,1)} %bitcast.17, bf16[27,32,32]{2,1,0:T(8,128)(2,1)} %bitcast.19, bf16[27,32,32]{2,1,0:T(8,128)(2,1)} %bitcast.20, bf16[32,8,8,128]{3,2,1,0:T(8,128)(2,1)} %bitcast.18), custom_call_target="tpu_custom_call" | custom-call | tf_op jit(solution)/shard_map/pallas_call | solution.py:546
  22.5 1.1 %shard_map.68 = (bf16[32,8,8,128]{3,2,1,0:T(8,128)(2,1)}, f32[27,32,32]{2,1,0:T(8,128)}, f32[27,32,32]{2,1,0:T(8,128)}) custom-call(bf16[32,8,8,128]{3,2,1,0:T(8,128)(2,1)S(1)} %get-tuple-element.8.out_ref, bf16[2,28,8,128]{3,2,1,0:T(8,128)(2,1)S(1)} %bitcast.16), custom_call_target="tpu_custom_call" | custom-call | tf_op jit(solution)/shard_map/pallas_call | solution.py:582
